TPU v7x, 32 devices: a whole 2x2x4 slice. The times are simulated.
32 devices in a mesh: dp: 4 (over y, core), head: 2 (over x), kv: 4 (over z).
Axes of the slice: x: 2, y: 2, z: 4, core: 2. Of those that a mesh axis runs over, the one named last changes fastest.
Arguments:
- teacher_query: bfloat16 [4, 1024, 3584], P('dp', 'kv', 'head'), may hold values from -96 to 96
- teacher_key: bfloat16 [4, 1024, 512], P('dp', 'kv', 'head'), may hold values from -8 to 8
- student_query: bfloat16 [4, 1024, 1792], P('dp', 'kv', 'head'), may hold values from -96 to 96
- student_key: bfloat16 [4, 1024, 256], P('dp', 'kv', 'head'), may hold values from -8 to 8
- pair_table: int32 [14, 2], replicated, may hold values from 0 to 27, as said below
Outputs:
- kl: float32 [4, 14, 1024], P('dp', 'head', 'kv')
- head_loss: float32 [14], P('head')
Inputs may be any that keep to these rules, and one draw needn't show every extreme that they name: `pair_table`: each of the 28 teacher heads appears exactly once in the table.
All inputs are finite; a program needn't handle non-finite values.
Results may differ from a plain program's by a relative error of at most 0.0003.
Values may be sent and summed in bfloat16 or wider, within the bound.
A program may use at most 64 MiB of HBM per device.

v0:
```python
import functools
import math

import jax
import jax.numpy as jnp
from jax import lax
from jax.experimental import pallas as pl
from jax.experimental.pallas import tpu as pltpu
from jax.sharding import PartitionSpec as P

HT = 28
KVT = 4
DH = 128
HS = 14
KVS = 2

MESH = pl.DeviceIdType.MESH
LOWEST = -1e30


def nn(a, b):
    return jnp.dot(a, b, preferred_element_type=jnp.float32)


def flip(x):
    n = x.shape[1]
    eye = (
        lax.broadcasted_iota(jnp.int32, (n, n), 0) == lax.broadcasted_iota(jnp.int32, (n, n), 1)
    ).astype(jnp.bfloat16)
    out = lax.dot_general(eye, x, (((1,), (1,)), ((), ())), preferred_element_type=jnp.float32)
    return out.astype(jnp.bfloat16)


def kernel(
    n_dp, n_head, n_kv, rows,
    table, tq_hbm, tk_hbm, sq_hbm, sk_hbm,
    kl_ref, loss_ref,
    tq, tk, sq, sk,
    tq_t, sq_t, key_t, mixed, t_max, s_max, s_sum,
    inverse, acc, acc_in, sums_out, sums,
    load_sem, x_send, x_recv, z_send, z_recv, sum_send, sum_recv,
):
    n_t, n_s = HT // n_head, HS // n_head
    g_t, g_s = KVT // n_head, KVS // n_head
    per_t, per_s = HT // KVT, HS // KVS
    dp, hd, kv = lax.axis_index("dp"), lax.axis_index("head"), lax.axis_index("kv")
    n_rank = n_dp * n_head * n_kv
    rank = (dp * n_head + hd) * n_kv + kv
    scale = 1.0 / math.sqrt(DH)
    rate = scale * math.log2(math.e)

    loads = [
        pltpu.make_async_copy(sk_hbm.at[0], sk.at[hd, kv], load_sem.at[0]),
        pltpu.make_async_copy(tk_hbm.at[0], tk.at[kv], load_sem.at[1]),
        pltpu.make_async_copy(sq_hbm.at[0], sq.at[hd], load_sem.at[2]),
        pltpu.make_async_copy(tq_hbm.at[0], tq, load_sem.at[3]),
    ]
    for load in loads:
        load.start()

    barrier = pltpu.get_barrier_semaphore()

    def coordinates(peer):
        return (peer // (n_head * n_kv), peer // n_kv % n_head, peer % n_kv)

    def greet(peer, carry):
        @pl.when(peer != rank)
        def _():
            pl.semaphore_signal(
                barrier, inc=1, device_id=coordinates(peer), device_id_type=MESH
            )
        return carry

    lax.fori_loop(0, n_rank, greet, 0)

    entries = [table[k % 2, k // 2] for k in range(HT)]
    for t in range(n_t):
        found = jnp.int32(0)
        for k in range(HT):
            found = jnp.where(entries[k] == hd * n_t + t, k // 2, found)
        inverse[t] = found

    for load in loads:
        load.wait()
    pl.semaphore_wait(barrier, n_rank - 1)

    def across(slot, step, src, dst):
        return pltpu.make_async_remote_copy(
            src_ref=src, dst_ref=dst, send_sem=x_send.at[slot, step - 1],
            recv_sem=x_recv.at[slot, step - 1],
            device_id={"head": (hd + step) % n_head}, device_id_type=MESH,
        )

    def upward(block, piece):
        ref = tk.at[block] if piece is n_head else sk.at[piece, block]
        return pltpu.make_async_remote_copy(
            src_ref=ref, dst_ref=ref, send_sem=z_send.at[block, piece],
            recv_sem=z_recv.at[block, piece],
            device_id={"kv": jnp.minimum(kv + 1, n_kv - 1)}, device_id_type=MESH,
        )

    def launch(piece):
        @pl.when(not_last)
        def _():
            upward(kv, piece).start()

    pieces = [n_head] + [(hd + s) % n_head for s in range(n_head)]
    not_last = kv < n_kv - 1

    keys_over = [across(0, s, sk.at[hd, kv], sk.at[hd, kv]) for s in range(1, n_head)]
    queries_over = [across(1, s, sq.at[hd], sq.at[hd]) for s in range(1, n_head)]
    for copy in keys_over:
        copy.start()

    launch(n_head)
    launch(hd)

    for copy in queries_over:
        copy.start()

    for h in range(n_t):
        tq_t[h] = flip(tq[:, h * DH:(h + 1) * DH])
    for h in range(n_s):
        sq_t[hd * n_s + h] = flip(sq[hd, :, h * DH:(h + 1) * DH])

    key_t[:, 2 * DH:] = jnp.ones((g_t * KVS, 16, rows), jnp.bfloat16)
    for copy in keys_over:
        copy.wait()

    for s in range(1, n_head):
        launch((hd + s) % n_head)

    visible = lax.broadcasted_iota(jnp.int32, (rows, rows), 0) <= lax.broadcasted_iota(
        jnp.int32, (rows, rows), 1
    )

    def fold(block, diagonal):
        for g in range(g_t):
            flipped = flip(tk[block, :, g * DH:(g + 1) * DH])
            for j in range(KVS):
                key_t[g * KVS + j, :DH] = flipped
        for j in range(KVS):
            flipped = flip(sk[j // g_s, block, :, j % g_s * DH:(j % g_s + 1) * DH])
            for g in range(g_t):
                key_t[g * KVS + j, DH:2 * DH] = flipped

        def weigh(logits, high, row):
            if diagonal:
                logits = jnp.where(visible, logits, LOWEST)
            top = jnp.max(logits, axis=0, keepdims=True)
            if diagonal:
                decay = None
            else:
                old = high[row]
                top = jnp.maximum(old, top)
                decay = jnp.exp2((old - top) * rate)
            weights = jnp.exp2((logits - top) * rate)
            high[row] = top
            return weights, decay

        for h in range(n_t):
            g = h // per_t
            logits = nn(tk[block, :, g * DH:(g + 1) * DH], tq_t[h])
            weights, decay = weigh(logits, t_max, h)
            part = nn(key_t[g * KVS + inverse[h] // per_s], weights.astype(jnp.bfloat16))
            mixed[h] = part if diagonal else mixed[h] * decay + part
        for h in range(n_s):
            g = h // per_s
            logits = nn(sk[hd, block, :, g * DH:(g + 1) * DH], sq_t[hd * n_s + h])
            weights, decay = weigh(logits, s_max, h)
            part = jnp.sum(weights, axis=0, keepdims=True)
            s_sum[h] = part if diagonal else s_sum[h] * decay + part

    fold(kv, True)

    def step(s, carry):
        block = kv - s
        for piece in pieces:
            upward(block, piece).wait_recv()

            @pl.when(not_last)
            def _():
                upward(block, piece).start()
        fold(block, False)
        return carry

    lax.fori_loop(1, kv + 1, step, 0)

    for copy in queries_over:
        copy.wait()
    for s in range(1, n_head):
        d = (hd + s) % n_head
        for h in range(n_s):
            sq_t[d * n_s + h] = flip(sq[d, :, h * DH:(h + 1) * DH])

    pad = acc.shape[0] // n_head
    place = lax.broadcasted_iota(jnp.int32, acc.shape, 0)
    total = jnp.zeros(acc.shape, jnp.float32)
    for h in range(n_t):
        partner = inverse[h]
        own = mixed[h, :DH] * tq_t[h].astype(jnp.float32)
        other = mixed[h, DH:2 * DH] * sq_t[partner].astype(jnp.float32)
        mass = mixed[h, 2 * DH:2 * DH + 1]
        value = jnp.sum(own - other, axis=0, keepdims=True) * scale / mass
        value = value - (t_max[h] * scale + jnp.log(mass))
        row = (partner // n_s) * pad + partner % n_s
        total = total + jnp.where(place == row, value, 0.0)
    acc[...] = total

    returns = [
        across(2, s, acc.at[pl.ds(((hd + s) % n_head) * pad, pad)], acc_in.at[s - 1])
        for s in range(1, n_head)
    ]
    for copy in returns:
        copy.start()
    lse = jnp.concatenate(
        [s_max[h] * scale + jnp.log(s_sum[h]) for h in range(n_s)]
        + [jnp.zeros((1, rows), jnp.float32)] * (pad - n_s),
        axis=0,
    )
    mine = jnp.where(place // pad == hd, 2.0 * jnp.concatenate([lse] * n_head, axis=0), 0.0)
    column = jnp.sum(total + mine, axis=1, keepdims=True)
    across_lanes = lax.broadcasted_iota(jnp.int32, (n_head * pad, 128), 1)
    down_rows = lax.broadcasted_iota(jnp.int32, (n_head * pad, 128), 0)
    for d in range(n_head):
        sums_out[d] = jnp.sum(
            jnp.where(down_rows == across_lanes + d * pad, column, 0.0), axis=0, keepdims=True
        )

    def share(peer, place):
        return pltpu.make_async_remote_copy(
            src_ref=sums_out.at[peer // n_kv % n_head], dst_ref=sums.at[rank],
            send_sem=sum_send.at[peer], recv_sem=sum_recv.at[place],
            device_id=coordinates(peer), device_id_type=MESH,
        )

    def send(peer, carry):
        @pl.when(peer != rank)
        def _():
            share(peer, rank).start()
        return carry

    def land(peer, carry):
        @pl.when(peer != rank)
        def _():
            share(peer, rank).wait_send()
            share(peer, peer).wait_recv()
        return carry

    lax.fori_loop(0, n_rank, send, 0)
    sums[rank] = sums_out[hd]
    kl = acc[pl.ds(hd * pad, pad)] + 2.0 * lse
    for s in range(1, n_head):
        returns[s - 1].wait()
        kl = kl + acc_in[s - 1]
    for h in range(n_s):
        kl_ref[h] = kl[h:h + 1]

    @pl.when(not_last)
    def _():
        def drain(block, carry):
            for piece in pieces:
                upward(block, piece).wait_send()
            return carry
        lax.fori_loop(0, kv + 1, drain, 0)

    lax.fori_loop(0, n_rank, land, 0)
    line = jnp.sum(sums[...], axis=0)
    loss_ref[...] = line[:, :n_s] / (n_dp * rows * n_kv)


def finish(kl_in, loss_in, kl_ref, loss_ref):
    kl_ref[...] = kl_in[...]
    loss_ref[...] = loss_in[...]


def per_device(teacher_query, teacher_key, student_query, student_key, pair_table):
    n_dp, n_head, n_kv = lax.axis_size("dp"), lax.axis_size("head"), lax.axis_size("kv")
    seq_dev, rows, wide_t = teacher_query.shape
    assert seq_dev == 1
    n_t, n_s = HT // n_head, HS // n_head
    g_t, g_s = KVT // n_head, KVS // n_head
    n_rank = n_dp * n_head * n_kv
    pad = -(-n_s // 8) * 8
    f32, bf16 = jnp.float32, jnp.bfloat16
    dma = pltpu.SemaphoreType.DMA
    kl, loss = pl.pallas_call(
        functools.partial(kernel, n_dp, n_head, n_kv, rows),
        out_shape=(
            jax.ShapeDtypeStruct((n_s, 1, rows), f32),
            jax.ShapeDtypeStruct((1, n_s), f32),
        ),
        in_specs=[pl.BlockSpec(memory_space=pltpu.SMEM)]
        + [pl.BlockSpec(memory_space=pl.ANY)] * 4,
        out_specs=(
            pl.BlockSpec(memory_space=pltpu.VMEM),
            pl.BlockSpec(memory_space=pltpu.VMEM),
        ),
        scratch_shapes=[
            pltpu.VMEM((rows, wide_t), bf16),
            pltpu.VMEM((n_kv, rows, g_t * DH), bf16),
            pltpu.VMEM((n_head, rows, n_s * DH), bf16),
            pltpu.VMEM((n_head, n_kv, rows, g_s * DH), bf16),
            pltpu.VMEM((n_t, DH, rows), bf16),
            pltpu.VMEM((HS, DH, rows), bf16),
            pltpu.VMEM((g_t * KVS, 2 * DH + 16, rows), bf16),
            pltpu.VMEM((n_t, 2 * DH + 16, rows), f32),
            pltpu.VMEM((n_t, 1, rows), f32),
            pltpu.VMEM((n_s, 1, rows), f32),
            pltpu.VMEM((n_s, 1, rows), f32),
            pltpu.SMEM((n_t,), jnp.int32),
            pltpu.VMEM((n_head * pad, rows), f32),
            pltpu.VMEM((max(n_head - 1, 1), pad, rows), f32),
            pltpu.VMEM((n_head, 1, 128), f32),
            pltpu.VMEM((n_rank, 1, 128), f32),
            dma((4,)),
            dma((3, max(n_head - 1, 1))),
            dma((3, max(n_head - 1, 1))),
            dma((n_kv, n_head + 1)),
            dma((n_kv, n_head + 1)),
            dma((n_rank,)),
            dma((n_rank,)),
        ],
        compiler_params=pltpu.CompilerParams(collective_id=0, has_side_effects=True),
    )(pair_table.T, teacher_query, teacher_key, student_query, student_key)
    kl, loss = pl.pallas_call(
        finish,
        out_shape=(
            jax.ShapeDtypeStruct((n_s, 1, rows), f32),
            jax.ShapeDtypeStruct((1, n_s), f32),
        ),
        in_specs=[pl.BlockSpec(memory_space=pltpu.VMEM)] * 2,
        out_specs=(
            pl.BlockSpec(memory_space=pltpu.VMEM),
            pl.BlockSpec(memory_space=pltpu.VMEM),
        ),
    )(kl, loss)
    return kl.reshape(1, n_s, rows), loss.reshape(n_s)


def solution(mesh):
    split = P("dp", "kv", "head")
    return jax.shard_map(
        per_device,
        mesh=mesh,
        in_specs=(split, split, split, split, P()),
        out_specs=(P("dp", "head", "kv"), P("head")),
        check_vma=False,
    )
```

profile of v0, /device:TPU:0, one launch (start us, length us, event | category | flops | bytes accessed | tf_op | source)
XLA Modules:
  0.0 36.4 jit_solution(5913148939650604362)
XLA Ops:
  0.6 34.5 %shard_map.68 = (f32[7,1,256]{2,1,0:T(1,128)}, f32[1,7]{1,0:T(1,128)}) custom-call(s32[2,14]{1,0:T(2,128)} %bitcast.3, bf16[1,256,1792]{2,1,0:T(8,128)(2,1)} %tq_hbm.1, bf16[1,256,256]{2,1,0:T(8,128)(2,1)} %tk_hbm.1, bf16[1,256,896]{2,1,0:T(8,128)(2,1)} %sq_hbm.1, bf16[1,256,128]{2,1,0:T(8,128)(2,1)} %sk_hbm.1), custom_call_target="tpu_custom_call" | custom-call | tf_op jit(solution)/shard_map/pallas_call | solution.py:287
  35.1 1.3 %shard_map.69 = (f32[7,1,256]{2,1,0:T(1,128)}, f32[1,7]{1,0:T(1,128)}) custom-call(f32[7,1,256]{2,1,0:T(1,128)} %get-tuple-element.6.kl_in, f32[1,7]{1,0:T(1,128)} %get-tuple-element.7.loss_in), custom_call_target="tpu_custom_call" | custom-call | tf_op jit(solution)/shard_map/pallas_call | solution.py:326
where the time goes:
time: 36.6 us; the launch traced here: 36.4 us
  Pallas kernels  35.8 us (98%)
  between operations  0.64 us (2%)
    pallas_call x1, Pallas kernels, per_device(): pl.pallas_call(functools.partial(kernel, n_dp, n_head, n_kv, rows), out_s...  34.5 us
    pallas_call x1, Pallas kernels, per_device(): pl.pallas_call(finish, out_shape=(jax.ShapeDtypeStruct((n_s, 1, rows), f3...  1.3 us

commit v1 on v0

--- a/solution.py
+++ b/solution.py
@@ -33,12 +33,12 @@
 
 def kernel(
     n_dp, n_head, n_kv, rows,
-    table, tq_hbm, tk_hbm, sq_hbm, sk_hbm,
+    table_hbm, tq_hbm, tk_hbm, sq_hbm, sk_hbm,
     kl_ref, loss_ref,
     tq, tk, sq, sk,
     tq_t, sq_t, key_t, mixed, t_max, s_max, s_sum,
-    inverse, acc, acc_in, sums_out, sums,
-    load_sem, x_send, x_recv, z_send, z_recv, sum_send, sum_recv,
+    table, inverse, acc, acc_in, sums_out, sums,
+    layer_sem, chain_sem, load_sem, x_send, x_recv, z_send, z_recv, sum_send, sum_recv,
 ):
     n_t, n_s = HT // n_head, HS // n_head
     g_t, g_s = KVT // n_head, KVS // n_head
@@ -54,6 +54,7 @@
         pltpu.make_async_copy(tk_hbm.at[0], tk.at[kv], load_sem.at[1]),
         pltpu.make_async_copy(sq_hbm.at[0], sq.at[hd], load_sem.at[2]),
         pltpu.make_async_copy(tq_hbm.at[0], tq, load_sem.at[3]),
+        pltpu.make_async_copy(table_hbm, table, load_sem.at[4]),
     ]
     for load in loads:
         load.start()
@@ -63,26 +64,28 @@
     def coordinates(peer):
         return (peer // (n_head * n_kv), peer // n_kv % n_head, peer % n_kv)
 
-    def greet(peer, carry):
-        @pl.when(peer != rank)
-        def _():
-            pl.semaphore_signal(
-                barrier, inc=1, device_id=coordinates(peer), device_id_type=MESH
-            )
-        return carry
-
-    lax.fori_loop(0, n_rank, greet, 0)
-
-    entries = [table[k % 2, k // 2] for k in range(HT)]
-    for t in range(n_t):
-        found = jnp.int32(0)
-        for k in range(HT):
-            found = jnp.where(entries[k] == hd * n_t + t, k // 2, found)
-        inverse[t] = found
-
-    for load in loads:
+    def greet(sem, **peer):
+        pl.semaphore_signal(sem, inc=1, device_id=peer, device_id_type=MESH)
+
+    first, last = kv == 0, kv == n_kv - 1
+    for s in range(1, n_dp):
+        greet(barrier, dp=(dp + s) % n_dp)
+    for s in range(1, n_head):
+        greet(barrier, head=(hd + s) % n_head)
+
+    @pl.when(jnp.logical_not(first))
+    def _():
+        greet(barrier, kv=kv - 1)
+
+    @pl.when(jnp.logical_not(last))
+    def _():
+        greet(barrier, kv=kv + 1)
+
+    near = n_dp - 1 + n_head - 1 + (kv > 0).astype(jnp.int32) + (kv < n_kv - 1).astype(jnp.int32)
+
+    for load in loads[:4]:
         load.wait()
-    pl.semaphore_wait(barrier, n_rank - 1)
+    pl.semaphore_wait(barrier, near)
 
     def across(slot, step, src, dst):
         return pltpu.make_async_remote_copy(
@@ -118,6 +121,16 @@
     for copy in queries_over:
         copy.start()
 
+    for s in range(1, n_head):
+        greet(layer_sem, head=(hd + s) % n_head)
+    loads[4].wait()
+    entries = [table[k % 2, k // 2] for k in range(HT)]
+    for t in range(n_t):
+        found = jnp.int32(0)
+        for k in range(HT):
+            found = jnp.where(entries[k] == hd * n_t + t, k // 2, found)
+        inverse[t] = found
+
     for h in range(n_t):
         tq_t[h] = flip(tq[:, h * DH:(h + 1) * DH])
     for h in range(n_s):
@@ -129,6 +142,16 @@
 
     for s in range(1, n_head):
         launch((hd + s) % n_head)
+
+    pl.semaphore_wait(layer_sem, n_head - 1)
+
+    @pl.when(jnp.logical_not(first))
+    def _():
+        pl.semaphore_wait(chain_sem.at[0], 1)
+
+    @pl.when(jnp.logical_not(last))
+    def _():
+        greet(chain_sem.at[0], kv=kv + 1)
 
     visible = lax.broadcasted_iota(jnp.int32, (rows, rows), 0) <= lax.broadcasted_iota(
         jnp.int32, (rows, rows), 1
@@ -172,6 +195,14 @@
             s_sum[h] = part if diagonal else s_sum[h] * decay + part
 
     fold(kv, True)
+
+    @pl.when(jnp.logical_not(last))
+    def _():
+        pl.semaphore_wait(chain_sem.at[1], 1)
+
+    @pl.when(jnp.logical_not(first))
+    def _():
+        greet(chain_sem.at[1], kv=kv - 1)
 
     def step(s, carry):
         block = kv - s
@@ -290,8 +321,7 @@
             jax.ShapeDtypeStruct((n_s, 1, rows), f32),
             jax.ShapeDtypeStruct((1, n_s), f32),
         ),
-        in_specs=[pl.BlockSpec(memory_space=pltpu.SMEM)]
-        + [pl.BlockSpec(memory_space=pl.ANY)] * 4,
+        in_specs=[pl.BlockSpec(memory_space=pl.ANY)] * 5,
         out_specs=(
             pl.BlockSpec(memory_space=pltpu.VMEM),
             pl.BlockSpec(memory_space=pltpu.VMEM),
@@ -308,12 +338,15 @@
             pltpu.VMEM((n_t, 1, rows), f32),
             pltpu.VMEM((n_s, 1, rows), f32),
             pltpu.VMEM((n_s, 1, rows), f32),
+            pltpu.SMEM(pair_table.shape[::-1], jnp.int32),
             pltpu.SMEM((n_t,), jnp.int32),
             pltpu.VMEM((n_head * pad, rows), f32),
             pltpu.VMEM((max(n_head - 1, 1), pad, rows), f32),
             pltpu.VMEM((n_head, 1, 128), f32),
             pltpu.VMEM((n_rank, 1, 128), f32),
-            dma((4,)),
+            pltpu.SemaphoreType.REGULAR,
+            pltpu.SemaphoreType.REGULAR((2,)),
+            dma((5,)),
             dma((3, max(n_head - 1, 1))),
             dma((3, max(n_head - 1, 1))),
             dma((n_kv, n_head + 1)),

time: 36.6 us -> 36 us (0.984)
  Pallas kernels: 35.8 us -> 35.2 us
    pallas_call x1, Pallas kernels: 34.5 us -> 33.9 us  [per_device(): pl.pallas_call(functools.partial(kernel, n_dp, n_head, n_kv, rows), out_s...]
where the time goes in v1:
time: 36 us; the launch traced here: 35.8 us
  Pallas kernels  35.2 us (98%)
  between operations  0.64 us (2%)
    pallas_call x1, Pallas kernels, per_device(): pl.pallas_call(functools.partial(kernel, n_dp, n_head, n_kv, rows), out_s...  33.9 us
    pallas_call x1, Pallas kernels, per_device(): pl.pallas_call(finish, out_shape=(jax.ShapeDtypeStruct((n_s, 1, rows), f3...  1.3 us

profile of v1, /device:TPU:0, one launch (start us, length us, event | category | flops | bytes accessed | tf_op | source)
XLA Modules:
  0.0 35.8 jit_solution(5382351932708634605)
XLA Ops:
  0.6 33.9 %shard_map.68 = (f32[7,1,256]{2,1,0:T(1,128)}, f32[1,7]{1,0:T(1,128)}) custom-call(s32[2,14]{1,0:T(2,128)} %bitcast.3, bf16[1,256,1792]{2,1,0:T(8,128)(2,1)} %tq_hbm.1, bf16[1,256,256]{2,1,0:T(8,128)(2,1)} %tk_hbm.1, bf16[1,256,896]{2,1,0:T(8,128)(2,1)} %sq_hbm.1, bf16[1,256,128]{2,1,0:T(8,128)(2,1)} %sk_hbm.1), custom_call_target="tpu_custom_call" | custom-call | tf_op jit(solution)/shard_map/pallas_call | solution.py:318
  34.5 1.3 %shard_map.69 = (f32[7,1,256]{2,1,0:T(1,128)}, f32[1,7]{1,0:T(1,128)}) custom-call(f32[7,1,256]{2,1,0:T(1,128)} %get-tuple-element.6.kl_in, f32[1,7]{1,0:T(1,128)} %get-tuple-element.7.loss_in), custom_call_target="tpu_custom_call" | custom-call | tf_op jit(solution)/shard_map/pallas_call | solution.py:359

commit v2 on v1

v2 whole, which is shorter than its diff:
```python
import functools
import math

import jax
import jax.numpy as jnp
from jax import lax
from jax.experimental import pallas as pl
from jax.experimental.pallas import tpu as pltpu
from jax.sharding import PartitionSpec as P

HT = 28
KVT = 4
DH = 128
HS = 14
KVS = 2

MESH = pl.DeviceIdType.MESH
LOWEST = -1e30


def nn(a, b):
    return jnp.dot(a, b, preferred_element_type=jnp.float32)


def flip(x):
    n = x.shape[1]
    eye = (
        lax.broadcasted_iota(jnp.int32, (n, n), 0) == lax.broadcasted_iota(jnp.int32, (n, n), 1)
    ).astype(jnp.bfloat16)
    out = lax.dot_general(eye, x, (((1,), (1,)), ((), ())), preferred_element_type=jnp.float32)
    return out.astype(jnp.bfloat16)


def kernel(
    n_dp, n_head, n_kv, rows, shared,
    table_hbm, tq_hbm, tk_hbm, sq_hbm, sk_hbm,
    kl_ref, loss_ref,
    tq, tk, sq, sk,
    tq_t, sq_t, tk_t, sk_t, weights, mixed_t, mixed_s, t_max, t_decay, s_max, s_sum,
    table, inverse, acc, acc_in, sums_out, sums,
    layer_sem, chain_sem, load_sem, key_send, key_recv, query_send, query_recv,
    back_send, back_recv, z_send, z_recv, sum_send, sum_recv,
):
    n_t, n_s = HT // n_head, HS // n_head
    g_t, g_s = KVT // n_head, KVS // n_head
    per_t, per_s = HT // KVT, HS // KVS
    dp, hd, kv = lax.axis_index("dp"), lax.axis_index("head"), lax.axis_index("kv")
    n_rank = n_dp * n_head * n_kv
    rank = (dp * n_head + hd) * n_kv + kv
    scale = 1.0 / math.sqrt(DH)
    rate = scale * math.log2(math.e)
    bf16 = jnp.bfloat16

    loads = [
        pltpu.make_async_copy(sk_hbm.at[0], sk.at[hd, kv], load_sem.at[0]),
        pltpu.make_async_copy(tk_hbm.at[0], tk.at[kv], load_sem.at[1]),
        pltpu.make_async_copy(sq_hbm.at[0], sq.at[hd], load_sem.at[2]),
        pltpu.make_async_copy(table_hbm, table, load_sem.at[3]),
        pltpu.make_async_copy(tq_hbm.at[0], tq, load_sem.at[4]),
    ]
    for load in loads:
        load.start()

    first, last = kv == 0, kv == n_kv - 1
    not_first, not_last = kv > 0, kv < n_kv - 1
    barrier = pltpu.get_barrier_semaphore()

    def greet(sem, **peer):
        pl.semaphore_signal(sem, inc=1, device_id=peer, device_id_type=MESH)

    @pl.when(not_first)
    def _():
        greet(barrier, kv=kv - 1)

    @pl.when(not_last)
    def _():
        greet(barrier, kv=kv + 1)

    for s in range(1, n_head):
        greet(barrier, head=(hd + s) % n_head)
    for s in range(1, n_dp):
        greet(barrier, dp=(dp + s) % n_dp)

    def column(step):
        return (hd + step) % n_head

    def across(step, src, dst, send, recv):
        return pltpu.make_async_remote_copy(
            src_ref=src, dst_ref=dst, send_sem=send, recv_sem=recv,
            device_id={"head": column(step)}, device_id_type=MESH,
        )

    def keys_over(block):
        return [
            across(
                s, sk.at[hd, block], sk.at[hd, block],
                key_send.at[block, s - 1], key_recv.at[block, s - 1],
            )
            for s in range(1, n_head)
        ]

    cuts = [0, n_s * 2 // 7, n_s * 4 // 7, n_s]
    n_group = len(cuts) - 1

    def queries_over(group):
        part = sq.at[hd, :, cuts[group] * DH:cuts[group + 1] * DH]
        return [
            across(s, part, part, query_send.at[group, s - 1], query_recv.at[group, s - 1])
            for s in range(1, n_head)
        ]

    def start(copies):
        for copy in copies:
            copy.start()

    def upward(block, piece):
        ref = tk.at[block] if piece == n_head else sk.at[column(piece), block]
        return pltpu.make_async_remote_copy(
            src_ref=ref, dst_ref=ref, send_sem=z_send.at[block, piece],
            recv_sem=z_recv.at[block, piece],
            device_id={"kv": jnp.minimum(kv + 1, n_kv - 1)}, device_id_type=MESH,
        )

    def launch(block, piece):
        @pl.when(not_last)
        def _():
            upward(block, piece).start()

    def land(block, piece):
        upward(block, piece).wait_recv()
        launch(block, piece)

    def receive_own(block):
        @pl.when(block >= shared)
        def _():
            land(block, 0)
            start(keys_over(block))

    def receive_rest(block):
        land(block, n_head)

        @pl.when(block < shared)
        def _():
            land(block, 0)
            for s in range(1, n_head):
                land(block, s)

    loads[0].wait()
    loads[1].wait()
    pl.semaphore_wait(
        barrier, n_dp - 1 + n_head - 1 + not_first.astype(jnp.int32) + not_last.astype(jnp.int32)
    )
    start(keys_over(kv))

    @pl.when(kv < shared)
    def _():
        launch(kv, n_head)
        launch(kv, 0)

    @pl.when(kv >= shared)
    def _():
        launch(kv, 0)
        launch(kv, n_head)

    loads[2].wait()
    start(queries_over(0))
    for s in range(1, n_head):
        greet(layer_sem, head=column(s))

    loads[3].wait()
    entries = [table[k % 2, k // 2] for k in range(HT)]
    for t in range(n_t):
        found = jnp.int32(0)
        for k in range(HT):
            found = jnp.where(entries[k] == hd * n_t + t, k // 2, found)
        inverse[t] = found

    loads[4].wait()
    for h in range(n_t):
        tq_t[h] = flip(tq[:, h * DH:(h + 1) * DH])
    for h in range(n_s):
        sq_t[hd * n_s + h] = flip(sq[hd, :, h * DH:(h + 1) * DH])
    tk_t[:, DH:] = jnp.ones((g_t, 16, rows), bf16)

    for copy in keys_over(kv):
        copy.wait_recv()

    @pl.when(kv < shared)
    def _():
        for s in range(1, n_head):
            launch(kv, s)

    @pl.when(not_last & not_first)
    def _():
        receive_own(kv - 1)
        receive_rest(kv - 1)

    pl.semaphore_wait(layer_sem, n_head - 1)

    @pl.when(not_first)
    def _():
        pl.semaphore_wait(chain_sem.at[0], 1)

    @pl.when(not_last)
    def _():
        greet(chain_sem.at[0], kv=kv + 1)

    visible = lax.broadcasted_iota(jnp.int32, (rows, rows), 0) <= lax.broadcasted_iota(
        jnp.int32, (rows, rows), 1
    )

    def fold(block, diagonal, between):
        def weigh(logits, high, row):
            if diagonal:
                logits = jnp.where(visible, logits, LOWEST)
            top = jnp.max(logits, axis=0, keepdims=True)
            if diagonal:
                decay = None
            else:
                old = high[row]
                top = jnp.maximum(old, top)
                decay = jnp.exp2((old - top) * rate)
            high[row] = top
            return jnp.exp2((logits - top) * rate), decay

        if not diagonal:
            @pl.when(last)
            def _():
                upward(block, n_head).wait_recv()

        for g in range(g_t):
            tk_t[g, :DH] = flip(tk[block, :, g * DH:(g + 1) * DH])
        for h in range(n_t):
            g = h // per_t
            logits = nn(tk[block, :, g * DH:(g + 1) * DH], tq_t[h])
            weight, decay = weigh(logits, t_max, h)
            weight = weight.astype(bf16)
            weights[h] = weight
            part = nn(tk_t[g], weight)
            if diagonal:
                mixed_t[h] = part
            else:
                t_decay[h] = decay
                mixed_t[h] = mixed_t[h] * decay + part

        between()
        if not diagonal:
            @pl.when(last & (block < shared))
            def _():
                upward(block, 0).wait_recv()

        for h in range(n_s):
            g = h // per_s
            logits = nn(sk[hd, block, :, g * DH:(g + 1) * DH], sq_t[hd * n_s + h])
            weight, decay = weigh(logits, s_max, h)
            part = jnp.sum(weight, axis=0, keepdims=True)
            s_sum[h] = part if diagonal else s_sum[h] * decay + part

        if not diagonal:
            @pl.when(last & (block < shared))
            def _():
                for s in range(1, n_head):
                    upward(block, s).wait_recv()

            @pl.when(block >= shared)
            def _():
                for copy in keys_over(block):
                    copy.wait_recv()

        for j in range(KVS):
            sk_t[j] = flip(sk[j // g_s, block, :, j % g_s * DH:(j % g_s + 1) * DH])
        for h in range(n_t):
            part = nn(sk_t[inverse[h] // per_s], weights[h])
            mixed_s[h] = part if diagonal else mixed_s[h] * t_decay[h] + part

    def after_own():
        @pl.when(last & not_first)
        def _():
            receive_own(kv - 1)

        start(queries_over(1))

        @pl.when(first)
        def _():
            start(queries_over(2))

    fold(kv, True, after_own)

    @pl.when(not_last)
    def _():
        pl.semaphore_wait(chain_sem.at[1], 1)

    @pl.when(not_first)
    def _():
        greet(chain_sem.at[1], kv=kv - 1)

    def step(s, carry):
        block = kv - s

        @pl.when(not_last & (s < kv))
        def _():
            receive_own(block - 1)
            receive_rest(block - 1)

        def between():
            @pl.when(last & (s < kv))
            def _():
                receive_own(block - 1)

            @pl.when(s == 1)
            def _():
                start(queries_over(2))

        fold(block, False, between)
        return carry

    lax.fori_loop(1, kv + 1, step, 0)

    for group in range(n_group):
        for copy in queries_over(group):
            copy.wait_recv()
        for s in range(1, n_head):
            for h in range(cuts[group], cuts[group + 1]):
                sq_t[column(s) * n_s + h] = flip(sq[column(s), :, h * DH:(h + 1) * DH])

    pad = acc.shape[0] // n_head
    place = lax.broadcasted_iota(jnp.int32, acc.shape, 0)
    total = jnp.zeros(acc.shape, jnp.float32)
    for h in range(n_t):
        partner = inverse[h]
        own = mixed_t[h, :DH] * tq_t[h].astype(jnp.float32)
        other = mixed_s[h] * sq_t[partner].astype(jnp.float32)
        mass = mixed_t[h, DH:DH + 1]
        value = jnp.sum(own - other, axis=0, keepdims=True) * scale / mass
        value = value - (t_max[h] * scale + jnp.log(mass))
        row = (partner // n_s) * pad + partner % n_s
        total = total + jnp.where(place == row, value, 0.0)
    acc[...] = total

    returns = [
        across(
            s, acc.at[pl.ds(column(s) * pad, pad)], acc_in.at[s - 1],
            back_send.at[s - 1], back_recv.at[s - 1],
        )
        for s in range(1, n_head)
    ]
    start(returns)
    lse = jnp.concatenate(
        [s_max[h] * scale + jnp.log(s_sum[h]) for h in range(n_s)]
        + [jnp.zeros((1, rows), jnp.float32)] * (pad - n_s),
        axis=0,
    )
    mine = jnp.where(place // pad == hd, 2.0 * jnp.concatenate([lse] * n_head, axis=0), 0.0)
    side = jnp.sum(total + mine, axis=1, keepdims=True)
    across_lanes = lax.broadcasted_iota(jnp.int32, (n_head * pad, 128), 1)
    down_rows = lax.broadcasted_iota(jnp.int32, (n_head * pad, 128), 0)
    for d in range(n_head):
        sums_out[d] = jnp.sum(
            jnp.where(down_rows == across_lanes + d * pad, side, 0.0), axis=0, keepdims=True
        )

    def share(d, h, k):
        return pltpu.make_async_remote_copy(
            src_ref=sums_out.at[h], dst_ref=sums.at[rank],
            send_sem=sum_send, recv_sem=sum_recv,
            device_id=(d, h, k), device_id_type=MESH,
        )

    def each_peer(act):
        def outer(k, carry):
            def middle(d, carry):
                for h in range(n_head):
                    @pl.when((d * n_head + h) * n_kv + k != rank)
                    def _():
                        act(d, h, k)
                return carry
            return lax.fori_loop(0, n_dp, middle, carry)
        lax.fori_loop(0, n_kv, outer, 0)

    each_peer(lambda d, h, k: share(d, h, k).start())
    sums[rank] = sums_out[hd]
    kl = acc[pl.ds(hd * pad, pad)] + 2.0 * lse
    for s in range(1, n_head):
        returns[s - 1].wait()
        kl = kl + acc_in[s - 1]
    for h in range(n_s):
        kl_ref[h] = kl[h:h + 1]

    for group in range(n_group):
        for copy in queries_over(group):
            copy.wait_send()

    def drain(block, carry):
        @pl.when((block >= shared) | (block == kv))
        def _():
            for copy in keys_over(block):
                copy.wait_send()

        @pl.when(not_last)
        def _():
            upward(block, 0).wait_send()
            upward(block, n_head).wait_send()

            @pl.when(block < shared)
            def _():
                for s in range(1, n_head):
                    upward(block, s).wait_send()
        return carry

    lax.fori_loop(0, kv + 1, drain, 0)

    others = sums.at[pl.ds(0, n_rank - 1)]
    pltpu.make_async_remote_copy(
        src_ref=others, dst_ref=others, send_sem=sum_send, recv_sem=sum_recv,
        device_id={"head": column(1)}, device_id_type=MESH,
    ).wait()
    line = jnp.sum(sums[...], axis=0)
    loss_ref[...] = line[:, :n_s] / (n_dp * rows * n_kv)


def finish(kl_in, loss_in, kl_ref, loss_ref):
    kl_ref[...] = kl_in[...]
    loss_ref[...] = loss_in[...]


def per_device(teacher_query, teacher_key, student_query, student_key, pair_table):
    n_dp, n_head, n_kv = lax.axis_size("dp"), lax.axis_size("head"), lax.axis_size("kv")
    seq_dev, rows, wide_t = teacher_query.shape
    assert seq_dev == 1
    n_t, n_s = HT // n_head, HS // n_head
    g_t, g_s = KVT // n_head, KVS // n_head
    n_rank = n_dp * n_head * n_kv
    pad = -(-n_s // 8) * 8
    key_t, key_s, query_s = g_t * DH, g_s * DH, n_s * DH
    spare = query_s + n_kv * key_s - (n_kv - 1) * (key_t + key_s)
    shared = min(max(round(spare / (2 * key_s * max(n_head - 1, 1))), 0), n_kv - 1)
    f32, bf16 = jnp.float32, jnp.bfloat16
    dma = pltpu.SemaphoreType.DMA
    kl, loss = pl.pallas_call(
        functools.partial(kernel, n_dp, n_head, n_kv, rows, shared),
        out_shape=(
            jax.ShapeDtypeStruct((n_s, 1, rows), f32),
            jax.ShapeDtypeStruct((1, n_s), f32),
        ),
        in_specs=[pl.BlockSpec(memory_space=pl.ANY)] * 5,
        out_specs=(
            pl.BlockSpec(memory_space=pltpu.VMEM),
            pl.BlockSpec(memory_space=pltpu.VMEM),
        ),
        scratch_shapes=[
            pltpu.VMEM((rows, wide_t), bf16),
            pltpu.VMEM((n_kv, rows, g_t * DH), bf16),
            pltpu.VMEM((n_head, rows, n_s * DH), bf16),
            pltpu.VMEM((n_head, n_kv, rows, g_s * DH), bf16),
            pltpu.VMEM((n_t, DH, rows), bf16),
            pltpu.VMEM((HS, DH, rows), bf16),
            pltpu.VMEM((g_t, DH + 16, rows), bf16),
            pltpu.VMEM((KVS, DH, rows), bf16),
            pltpu.VMEM((n_t, rows, rows), bf16),
            pltpu.VMEM((n_t, DH + 16, rows), f32),
            pltpu.VMEM((n_t, DH, rows), f32),
            pltpu.VMEM((n_t, 1, rows), f32),
            pltpu.VMEM((n_t, 1, rows), f32),
            pltpu.VMEM((n_s, 1, rows), f32),
            pltpu.VMEM((n_s, 1, rows), f32),
            pltpu.SMEM(pair_table.shape[::-1], jnp.int32),
            pltpu.SMEM((n_t,), jnp.int32),
            pltpu.VMEM((n_head * pad, rows), f32),
            pltpu.VMEM((max(n_head - 1, 1), pad, rows), f32),
            pltpu.VMEM((n_head, 1, 128), f32),
            pltpu.VMEM((n_rank, 1, 128), f32),
            pltpu.SemaphoreType.REGULAR,
            pltpu.SemaphoreType.REGULAR((2,)),
            dma((5,)),
            dma((n_kv, max(n_head - 1, 1))),
            dma((n_kv, max(n_head - 1, 1))),
            dma((3, max(n_head - 1, 1))),
            dma((3, max(n_head - 1, 1))),
            dma((max(n_head - 1, 1),)),
            dma((max(n_head - 1, 1),)),
            dma((n_kv, n_head + 1)),
            dma((n_kv, n_head + 1)),
            dma(()),
            dma(()),
        ],
        compiler_params=pltpu.CompilerParams(collective_id=0, has_side_effects=True),
    )(pair_table.T, teacher_query, teacher_key, student_query, student_key)
    kl, loss = pl.pallas_call(
        finish,
        out_shape=(
            jax.ShapeDtypeStruct((n_s, 1, rows), f32),
            jax.ShapeDtypeStruct((1, n_s), f32),
        ),
        in_specs=[pl.BlockSpec(memory_space=pltpu.VMEM)] * 2,
        out_specs=(
            pl.BlockSpec(memory_space=pltpu.VMEM),
            pl.BlockSpec(memory_space=pltpu.VMEM),
        ),
    )(kl, loss)
    return kl.reshape(1, n_s, rows), loss.reshape(n_s)


def solution(mesh):
    split = P("dp", "kv", "head")
    return jax.shard_map(
        per_device,
        mesh=mesh,
        in_specs=(split, split, split, split, P()),
        out_specs=(P("dp", "head", "kv"), P("head")),
        check_vma=False,
    )
```

time: 36 us -> 42.8 us (1.19)
  Pallas kernels: 35.2 us -> 42 us
    pallas_call x1, Pallas kernels: 33.9 us -> 40.7 us  [per_device(): pl.pallas_call(functools.partial(kernel, n_dp, n_head, n_kv, rows, shared...]
where the time goes in v2:
time: 42.8 us; the launch traced here: 42.6 us
  Pallas kernels  42 us (98%)
  between operations  0.64 us (1%)
    pallas_call x1, Pallas kernels, per_device(): pl.pallas_call(functools.partial(kernel, n_dp, n_head, n_kv, rows, shared...  40.7 us
    pallas_call x1, Pallas kernels, per_device(): pl.pallas_call(finish, out_shape=(jax.ShapeDtypeStruct((n_s, 1, rows), f3...  1.3 us

profile of v2, /device:TPU:0, one launch (start us, length us, event | category | flops | bytes accessed | tf_op | source)
XLA Modules:
  0.0 42.6 jit_solution(4532535383059262445)
XLA Ops:
  0.6 40.7 %shard_map.68 = (f32[7,1,256]{2,1,0:T(1,128)}, f32[1,7]{1,0:T(1,128)}) custom-call(s32[2,14]{1,0:T(2,128)} %bitcast.3, bf16[1,256,1792]{2,1,0:T(8,128)(2,1)} %tq_hbm.1, bf16[1,256,256]{2,1,0:T(8,128)(2,1)} %tk_hbm.1, bf16[1,256,896]{2,1,0:T(8,128)(2,1)} %sq_hbm.1, bf16[1,256,128]{2,1,0:T(8,128)(2,1)} %sk_hbm.1), custom_call_target="tpu_custom_call" | custom-call | tf_op jit(solution)/shard_map/pallas_call | solution.py:439
  41.3 1.3 %shard_map.69 = (f32[7,1,256]{2,1,0:T(1,128)}, f32[1,7]{1,0:T(1,128)}) custom-call(f32[7,1,256]{2,1,0:T(1,128)} %get-tuple-element.6.kl_in, f32[1,7]{1,0:T(1,128)} %get-tuple-element.7.loss_in), custom_call_target="tpu_custom_call" | custom-call | tf_op jit(solution)/shard_map/pallas_call | solution.py:488

commit v3 on v2

--- a/solution.py
+++ b/solution.py
@@ -36,7 +36,7 @@
     table_hbm, tq_hbm, tk_hbm, sq_hbm, sk_hbm,
     kl_ref, loss_ref,
     tq, tk, sq, sk,
-    tq_t, sq_t, tk_t, sk_t, weights, mixed_t, mixed_s, t_max, t_decay, s_max, s_sum,
+    tq_t, sq_t, key_t, weights, mixed, t_max, t_decay, s_max, s_sum,
     table, inverse, acc, acc_in, sums_out, sums,
     layer_sem, chain_sem, load_sem, key_send, key_recv, query_send, query_recv,
     back_send, back_recv, z_send, z_recv, sum_send, sum_recv,
@@ -180,7 +180,8 @@
         tq_t[h] = flip(tq[:, h * DH:(h + 1) * DH])
     for h in range(n_s):
         sq_t[hd * n_s + h] = flip(sq[hd, :, h * DH:(h + 1) * DH])
-    tk_t[:, DH:] = jnp.ones((g_t, 16, rows), bf16)
+    key_t[:, 2 * DH:] = jnp.ones((g_t * KVS, 16, rows), bf16)
+    mixed[...] = jnp.zeros(mixed.shape, jnp.float32)
 
     for copy in keys_over(kv):
         copy.wait_recv()
@@ -209,41 +210,41 @@
         jnp.int32, (rows, rows), 1
     )
 
-    def fold(block, diagonal, between):
-        def weigh(logits, high, row):
-            if diagonal:
-                logits = jnp.where(visible, logits, LOWEST)
-            top = jnp.max(logits, axis=0, keepdims=True)
-            if diagonal:
-                decay = None
-            else:
-                old = high[row]
-                top = jnp.maximum(old, top)
-                decay = jnp.exp2((old - top) * rate)
-            high[row] = top
-            return jnp.exp2((logits - top) * rate), decay
-
+    def weigh(logits, high, row, diagonal):
+        if diagonal:
+            logits = jnp.where(visible, logits, LOWEST)
+        top = jnp.max(logits, axis=0, keepdims=True)
+        if diagonal:
+            decay = jnp.zeros_like(top)
+        else:
+            old = high[row]
+            top = jnp.maximum(old, top)
+            decay = jnp.exp2((old - top) * rate)
+        high[row] = top
+        return jnp.exp2((logits - top) * rate), decay
+
+    def turn_student(c, block):
+        for j in range(g_s):
+            flipped = flip(sk[c, block, :, j * DH:(j + 1) * DH])
+            for g in range(g_t):
+                key_t[g * KVS + c * g_s + j, DH:2 * DH] = flipped
+
+    def weigh_block(block, diagonal):
         if not diagonal:
             @pl.when(last)
             def _():
                 upward(block, n_head).wait_recv()
 
-        for g in range(g_t):
-            tk_t[g, :DH] = flip(tk[block, :, g * DH:(g + 1) * DH])
         for h in range(n_t):
             g = h // per_t
             logits = nn(tk[block, :, g * DH:(g + 1) * DH], tq_t[h])
-            weight, decay = weigh(logits, t_max, h)
-            weight = weight.astype(bf16)
-            weights[h] = weight
-            part = nn(tk_t[g], weight)
-            if diagonal:
-                mixed_t[h] = part
-            else:
-                t_decay[h] = decay
-                mixed_t[h] = mixed_t[h] * decay + part
-
-        between()
+            weight, t_decay[h] = weigh(logits, t_max, h, diagonal)
+            weights[h] = weight.astype(bf16)
+        for g in range(g_t):
+            flipped = flip(tk[block, :, g * DH:(g + 1) * DH])
+            for j in range(KVS):
+                key_t[g * KVS + j, :DH] = flipped
+
         if not diagonal:
             @pl.when(last & (block < shared))
             def _():
@@ -252,26 +253,28 @@
         for h in range(n_s):
             g = h // per_s
             logits = nn(sk[hd, block, :, g * DH:(g + 1) * DH], sq_t[hd * n_s + h])
-            weight, decay = weigh(logits, s_max, h)
+            weight, decay = weigh(logits, s_max, h, diagonal)
             part = jnp.sum(weight, axis=0, keepdims=True)
             s_sum[h] = part if diagonal else s_sum[h] * decay + part
-
-        if not diagonal:
-            @pl.when(last & (block < shared))
-            def _():
-                for s in range(1, n_head):
-                    upward(block, s).wait_recv()
-
-            @pl.when(block >= shared)
-            def _():
-                for copy in keys_over(block):
-                    copy.wait_recv()
-
-        for j in range(KVS):
-            sk_t[j] = flip(sk[j // g_s, block, :, j % g_s * DH:(j % g_s + 1) * DH])
-        for h in range(n_t):
-            part = nn(sk_t[inverse[h] // per_s], weights[h])
-            mixed_s[h] = part if diagonal else mixed_s[h] * t_decay[h] + part
+        turn_student(hd, block)
+
+    def await_others(block):
+        @pl.when((block < shared) & last & not_first & (block != kv))
+        def _():
+            for s in range(1, n_head):
+                upward(block, s).wait_recv()
+
+        @pl.when((block >= shared) & (block != kv))
+        def _():
+            for copy in keys_over(block):
+                copy.wait_recv()
+
+        for s in range(1, n_head):
+            turn_student(column(s), block)
+
+    def mix(h):
+        part = nn(key_t[h // per_t * KVS + inverse[h] // per_s], weights[h])
+        return mixed[h] * t_decay[h] + part
 
     def after_own():
         @pl.when(last & not_first)
@@ -284,7 +287,8 @@
         def _():
             start(queries_over(2))
 
-    fold(kv, True, after_own)
+    weigh_block(kv, True)
+    after_own()
 
     @pl.when(not_last)
     def _():
@@ -302,16 +306,19 @@
             receive_own(block - 1)
             receive_rest(block - 1)
 
-        def between():
-            @pl.when(last & (s < kv))
-            def _():
-                receive_own(block - 1)
-
-            @pl.when(s == 1)
-            def _():
-                start(queries_over(2))
-
-        fold(block, False, between)
+        await_others(block + 1)
+        for h in range(n_t):
+            mixed[h] = mix(h)
+        weigh_block(block, False)
+
+        @pl.when(last & (s < kv))
+        def _():
+            receive_own(block - 1)
+
+        @pl.when(s == 1)
+        def _():
+            start(queries_over(2))
+
         return carry
 
     lax.fori_loop(1, kv + 1, step, 0)
@@ -323,14 +330,16 @@
             for h in range(cuts[group], cuts[group + 1]):
                 sq_t[column(s) * n_s + h] = flip(sq[column(s), :, h * DH:(h + 1) * DH])
 
+    await_others(0)
     pad = acc.shape[0] // n_head
     place = lax.broadcasted_iota(jnp.int32, acc.shape, 0)
     total = jnp.zeros(acc.shape, jnp.float32)
     for h in range(n_t):
         partner = inverse[h]
-        own = mixed_t[h, :DH] * tq_t[h].astype(jnp.float32)
-        other = mixed_s[h] * sq_t[partner].astype(jnp.float32)
-        mass = mixed_t[h, DH:DH + 1]
+        blend = mix(h)
+        own = blend[:DH] * tq_t[h].astype(jnp.float32)
+        other = blend[DH:2 * DH] * sq_t[partner].astype(jnp.float32)
+        mass = blend[2 * DH:2 * DH + 1]
         value = jnp.sum(own - other, axis=0, keepdims=True) * scale / mass
         value = value - (t_max[h] * scale + jnp.log(mass))
         row = (partner // n_s) * pad + partner % n_s
@@ -454,11 +463,9 @@
             pltpu.VMEM((n_head, n_kv, rows, g_s * DH), bf16),
             pltpu.VMEM((n_t, DH, rows), bf16),
             pltpu.VMEM((HS, DH, rows), bf16),
-            pltpu.VMEM((g_t, DH + 16, rows), bf16),
-            pltpu.VMEM((KVS, DH, rows), bf16),
+            pltpu.VMEM((g_t * KVS, 2 * DH + 16, rows), bf16),
             pltpu.VMEM((n_t, rows, rows), bf16),
-            pltpu.VMEM((n_t, DH + 16, rows), f32),
-            pltpu.VMEM((n_t, DH, rows), f32),
+            pltpu.VMEM((n_t, 2 * DH + 16, rows), f32),
             pltpu.VMEM((n_t, 1, rows), f32),
             pltpu.VMEM((n_t, 1, rows), f32),
             pltpu.VMEM((n_s, 1, rows), f32),

time: 42.8 us -> 34.7 us (0.81)
  Pallas kernels: 42 us -> 33.9 us
    pallas_call x1, Pallas kernels: 40.7 us -> 32.6 us  [per_device(): pl.pallas_call(functools.partial(kernel, n_dp, n_head, n_kv, rows, shared...]
where the time goes in v3:
time: 34.7 us; the launch traced here: 34.5 us
  Pallas kernels  33.9 us (98%)
  between operations  0.64 us (2%)
    pallas_call x1, Pallas kernels, per_device(): pl.pallas_call(functools.partial(kernel, n_dp, n_head, n_kv, rows, shared...  32.6 us
    pallas_call x1, Pallas kernels, per_device(): pl.pallas_call(finish, out_shape=(jax.ShapeDtypeStruct((n_s, 1, rows), f3...  1.3 us

profile of v3, /device:TPU:0, one launch (start us, length us, event | category | flops | bytes accessed | tf_op | source)
XLA Modules:
  0.0 34.5 jit_solution(7985609588599758259)
XLA Ops:
  0.6 32.6 %shard_map.68 = (f32[7,1,256]{2,1,0:T(1,128)}, f32[1,7]{1,0:T(1,128)}) custom-call(s32[2,14]{1,0:T(2,128)} %bitcast.3, bf16[1,256,1792]{2,1,0:T(8,128)(2,1)} %tq_hbm.1, bf16[1,256,256]{2,1,0:T(8,128)(2,1)} %tk_hbm.1, bf16[1,256,896]{2,1,0:T(8,128)(2,1)} %sq_hbm.1, bf16[1,256,128]{2,1,0:T(8,128)(2,1)} %sk_hbm.1), custom_call_target="tpu_custom_call" | custom-call | tf_op jit(solution)/shard_map/pallas_call | solution.py:448
  33.2 1.3 %shard_map.69 = (f32[7,1,256]{2,1,0:T(1,128)}, f32[1,7]{1,0:T(1,128)}) custom-call(f32[7,1,256]{2,1,0:T(1,128)} %get-tuple-element.6.kl_in, f32[1,7]{1,0:T(1,128)} %get-tuple-element.7.loss_in), custom_call_target="tpu_custom_call" | custom-call | tf_op jit(solution)/shard_map/pallas_call | solution.py:495

commit v4 on v3

--- a/solution.py
+++ b/solution.py
@@ -99,7 +99,7 @@
             for s in range(1, n_head)
         ]
 
-    cuts = [0, n_s * 2 // 7, n_s * 4 // 7, n_s]
+    cuts = [0, n_s * 2 // 7, n_s * 5 // 7, n_s]
     n_group = len(cuts) - 1
 
     def queries_over(group):
@@ -183,11 +183,20 @@
     key_t[:, 2 * DH:] = jnp.ones((g_t * KVS, 16, rows), bf16)
     mixed[...] = jnp.zeros(mixed.shape, jnp.float32)
 
-    for copy in keys_over(kv):
-        copy.wait_recv()
+    pl.semaphore_wait(layer_sem, n_head - 1)
+    for way, inner in ((0, not_last), (1, not_first)):
+        @pl.when(not_first & not_last)
+        def _():
+            pl.semaphore_wait(chain_sem.at[way], 1)
+
+        @pl.when(inner)
+        def _():
+            greet(chain_sem.at[way], kv=kv + 1 - 2 * way)
 
     @pl.when(kv < shared)
     def _():
+        for copy in keys_over(kv):
+            copy.wait_recv()
         for s in range(1, n_head):
             launch(kv, s)
 
@@ -195,16 +204,6 @@
     def _():
         receive_own(kv - 1)
         receive_rest(kv - 1)
-
-    pl.semaphore_wait(layer_sem, n_head - 1)
-
-    @pl.when(not_first)
-    def _():
-        pl.semaphore_wait(chain_sem.at[0], 1)
-
-    @pl.when(not_last)
-    def _():
-        greet(chain_sem.at[0], kv=kv + 1)
 
     visible = lax.broadcasted_iota(jnp.int32, (rows, rows), 0) <= lax.broadcasted_iota(
         jnp.int32, (rows, rows), 1
@@ -264,7 +263,7 @@
             for s in range(1, n_head):
                 upward(block, s).wait_recv()
 
-        @pl.when((block >= shared) & (block != kv))
+        @pl.when(block >= shared)
         def _():
             for copy in keys_over(block):
                 copy.wait_recv()
@@ -289,14 +288,6 @@
 
     weigh_block(kv, True)
     after_own()
-
-    @pl.when(not_last)
-    def _():
-        pl.semaphore_wait(chain_sem.at[1], 1)
-
-    @pl.when(not_first)
-    def _():
-        greet(chain_sem.at[1], kv=kv - 1)
 
     def step(s, carry):
         block = kv - s
@@ -386,6 +377,11 @@
             return lax.fori_loop(0, n_dp, middle, carry)
         lax.fori_loop(0, n_kv, outer, 0)
 
+    for way, edge in ((0, last), (1, first)):
+        @pl.when(edge)
+        def _():
+            pl.semaphore_wait(chain_sem.at[way], 1)
+
     each_peer(lambda d, h, k: share(d, h, k).start())
     sums[rank] = sums_out[hd]
     kl = acc[pl.ds(hd * pad, pad)] + 2.0 * lse
@@ -425,11 +421,6 @@
     ).wait()
     line = jnp.sum(sums[...], axis=0)
     loss_ref[...] = line[:, :n_s] / (n_dp * rows * n_kv)
-
-
-def finish(kl_in, loss_in, kl_ref, loss_ref):
-    kl_ref[...] = kl_in[...]
-    loss_ref[...] = loss_in[...]
 
 
 def per_device(teacher_query, teacher_key, student_query, student_key, pair_table):
@@ -448,8 +439,8 @@
     kl, loss = pl.pallas_call(
         functools.partial(kernel, n_dp, n_head, n_kv, rows, shared),
         out_shape=(
-            jax.ShapeDtypeStruct((n_s, 1, rows), f32),
-            jax.ShapeDtypeStruct((1, n_s), f32),
+            pltpu.VMEM((n_s, 1, rows), f32),
+            pltpu.VMEM((1, n_s), f32),
         ),
         in_specs=[pl.BlockSpec(memory_space=pl.ANY)] * 5,
         out_specs=(
@@ -492,18 +483,6 @@
         ],
         compiler_params=pltpu.CompilerParams(collective_id=0, has_side_effects=True),
     )(pair_table.T, teacher_query, teacher_key, student_query, student_key)
-    kl, loss = pl.pallas_call(
-        finish,
-        out_shape=(
-            jax.ShapeDtypeStruct((n_s, 1, rows), f32),
-            jax.ShapeDtypeStruct((1, n_s), f32),
-        ),
-        in_specs=[pl.BlockSpec(memory_space=pltpu.VMEM)] * 2,
-        out_specs=(
-            pl.BlockSpec(memory_space=pltpu.VMEM),
-            pl.BlockSpec(memory_space=pltpu.VMEM),
-        ),
-    )(kl, loss)
     return kl.reshape(1, n_s, rows), loss.reshape(n_s)
 
 

time: 34.7 us -> 30.3 us (0.87)
  Pallas kernels: 33.9 us -> 28.4 us
  local copies, waits for them, and re-layouts: 0 us -> 1.11 us
    pallas_call x1, Pallas kernels: 32.6 us -> 28.4 us  [per_device(): pl.pallas_call(functools.partial(kernel, n_dp, n_head, n_kv, rows, shared...]
    pallas_call x1 -> x0, Pallas kernels: 1.3 us -> none  [per_device(): pl.pallas_call(finish, out_shape=(jax.ShapeDtypeStruct((n_s, 1, rows), f3...]
    unnamed x0 -> x2, local copies, waits for them, and re-layouts: none -> 1.11 us
where the time goes in v4:
time: 30.3 us; the launch traced here: 30.2 us
  Pallas kernels  28.4 us (94%)
  local copies, waits for them, and re-layouts  1.11 us (4%)
  between operations  0.64 us (2%)
    pallas_call x1, Pallas kernels, per_device(): pl.pallas_call(functools.partial(kernel, n_dp, n_head, n_kv, rows, shared...  28.4 us
    unnamed x2, local copies, waits for them, and re-layouts  1.11 us

profile of v4, /device:TPU:0, one launch (start us, length us, event | category | flops | bytes accessed | tf_op | source)
XLA Modules:
  0.0 30.2 jit_solution(13162774142286593677)
XLA Ops:
  0.6 28.4 %shard_map.68 = (f32[7,1,256]{2,1,0:T(1,128)S(1)}, f32[1,7]{1,0:T(1,128)S(1)}) custom-call(s32[2,14]{1,0:T(2,128)} %bitcast.5, bf16[1,256,1792]{2,1,0:T(8,128)(2,1)} %tq_hbm.1, bf16[1,256,256]{2,1,0:T(8,128)(2,1)} %tk_hbm.1, bf16[1,256,896]{2,1,0:T(8,128)(2,1)} %sq_hbm.1, bf16[1,256,128]{2,1,0:T(8,128)(2,1)} %sk_hbm.1), custom_call_target="tpu_custom_call" | custom-call | tf_op jit(solution)/shard_map/pallas_call | solution.py:439
  29.1 0.6 %copy.9 = f32[1,7,256]{2,0,1:T(1,128)} copy(f32[1,7,256]{2,0,1:T(1,128)S(1)} %bitcast.3) | data formatting | bytes 14336
  29.7 0.5 %copy.10 = f32[7]{0:T(128)} copy(f32[7]{0:T(128)S(1)} %bitcast.4) | data formatting | bytes 56

commit v5 on v4

--- a/solution.py
+++ b/solution.py
@@ -113,8 +113,14 @@
         for copy in copies:
             copy.start()
 
+    half = rows // 2
+    halves = (n_head, n_head + 1)
+
     def upward(block, piece):
-        ref = tk.at[block] if piece == n_head else sk.at[column(piece), block]
+        if piece < n_head:
+            ref = sk.at[column(piece), block]
+        else:
+            ref = tk.at[block, pl.ds((piece - n_head) * half, half)]
         return pltpu.make_async_remote_copy(
             src_ref=ref, dst_ref=ref, send_sem=z_send.at[block, piece],
             recv_sem=z_recv.at[block, piece],
@@ -137,7 +143,8 @@
             start(keys_over(block))
 
     def receive_rest(block):
-        land(block, n_head)
+        for piece in halves:
+            land(block, piece)
 
         @pl.when(block < shared)
         def _():
@@ -146,7 +153,6 @@
                 land(block, s)
 
     loads[0].wait()
-    loads[1].wait()
     pl.semaphore_wait(
         barrier, n_dp - 1 + n_head - 1 + not_first.astype(jnp.int32) + not_last.astype(jnp.int32)
     )
@@ -154,13 +160,17 @@
 
     @pl.when(kv < shared)
     def _():
-        launch(kv, n_head)
+        loads[1].wait()
+        for piece in halves:
+            launch(kv, piece)
         launch(kv, 0)
 
     @pl.when(kv >= shared)
     def _():
         launch(kv, 0)
-        launch(kv, n_head)
+        loads[1].wait()
+        for piece in halves:
+            launch(kv, piece)
 
     loads[2].wait()
     start(queries_over(0))
@@ -180,7 +190,7 @@
         tq_t[h] = flip(tq[:, h * DH:(h + 1) * DH])
     for h in range(n_s):
         sq_t[hd * n_s + h] = flip(sq[hd, :, h * DH:(h + 1) * DH])
-    key_t[:, 2 * DH:] = jnp.ones((g_t * KVS, 16, rows), bf16)
+    key_t[:, :, 2 * DH:] = jnp.ones((2, g_t * KVS, 16, rows), bf16)
     mixed[...] = jnp.zeros(mixed.shape, jnp.float32)
 
     pl.semaphore_wait(layer_sem, n_head - 1)
@@ -222,27 +232,28 @@
         high[row] = top
         return jnp.exp2((logits - top) * rate), decay
 
-    def turn_student(c, block):
+    def turn_student(c, block, slot):
         for j in range(g_s):
             flipped = flip(sk[c, block, :, j * DH:(j + 1) * DH])
             for g in range(g_t):
-                key_t[g * KVS + c * g_s + j, DH:2 * DH] = flipped
-
-    def weigh_block(block, diagonal):
+                key_t[slot, g * KVS + c * g_s + j, DH:2 * DH] = flipped
+
+    def weigh_block(block, slot, diagonal):
         if not diagonal:
             @pl.when(last)
             def _():
-                upward(block, n_head).wait_recv()
+                for piece in halves:
+                    upward(block, piece).wait_recv()
 
         for h in range(n_t):
             g = h // per_t
             logits = nn(tk[block, :, g * DH:(g + 1) * DH], tq_t[h])
-            weight, t_decay[h] = weigh(logits, t_max, h, diagonal)
-            weights[h] = weight.astype(bf16)
+            weight, t_decay[slot, h] = weigh(logits, t_max, h, diagonal)
+            weights[slot, h] = weight.astype(bf16)
         for g in range(g_t):
             flipped = flip(tk[block, :, g * DH:(g + 1) * DH])
             for j in range(KVS):
-                key_t[g * KVS + j, :DH] = flipped
+                key_t[slot, g * KVS + j, :DH] = flipped
 
         if not diagonal:
             @pl.when(last & (block < shared))
@@ -255,9 +266,9 @@
             weight, decay = weigh(logits, s_max, h, diagonal)
             part = jnp.sum(weight, axis=0, keepdims=True)
             s_sum[h] = part if diagonal else s_sum[h] * decay + part
-        turn_student(hd, block)
-
-    def await_others(block):
+        turn_student(hd, block, slot)
+
+    def await_others(block, slot):
         @pl.when((block < shared) & last & not_first & (block != kv))
         def _():
             for s in range(1, n_head):
@@ -269,11 +280,19 @@
                 copy.wait_recv()
 
         for s in range(1, n_head):
-            turn_student(column(s), block)
-
-    def mix(h):
-        part = nn(key_t[h // per_t * KVS + inverse[h] // per_s], weights[h])
-        return mixed[h] * t_decay[h] + part
+            turn_student(column(s), block, slot)
+
+    def mix(h, slot):
+        part = nn(key_t[slot, h // per_t * KVS + inverse[h] // per_s], weights[slot, h])
+        return mixed[h] * t_decay[slot, h] + part
+
+    def turn_queries(groups):
+        for group in groups:
+            for copy in queries_over(group):
+                copy.wait_recv()
+            for s in range(1, n_head):
+                for h in range(cuts[group], cuts[group + 1]):
+                    sq_t[column(s) * n_s + h] = flip(sq[column(s), :, h * DH:(h + 1) * DH])
 
     def after_own():
         @pl.when(last & not_first)
@@ -286,7 +305,7 @@
         def _():
             start(queries_over(2))
 
-    weigh_block(kv, True)
+    weigh_block(kv, 0, True)
     after_own()
 
     def step(s, carry):
@@ -297,37 +316,45 @@
             receive_own(block - 1)
             receive_rest(block - 1)
 
-        await_others(block + 1)
+        @pl.when((s == kv) & (s > 1))
+        def _():
+            turn_queries((0, 1))
+
+        weigh_block(block, s % 2, False)
+
+        @pl.when(last & (s < kv))
+        def _():
+            receive_own(block - 1)
+
+        @pl.when(s == 1)
+        def _():
+            start(queries_over(2))
+
+        await_others(block + 1, (s - 1) % 2)
         for h in range(n_t):
-            mixed[h] = mix(h)
-        weigh_block(block, False)
-
-        @pl.when(last & (s < kv))
-        def _():
-            receive_own(block - 1)
-
-        @pl.when(s == 1)
-        def _():
-            start(queries_over(2))
-
+            mixed[h] = mix(h, (s - 1) % 2)
         return carry
 
     lax.fori_loop(1, kv + 1, step, 0)
 
-    for group in range(n_group):
-        for copy in queries_over(group):
-            copy.wait_recv()
-        for s in range(1, n_head):
-            for h in range(cuts[group], cuts[group + 1]):
-                sq_t[column(s) * n_s + h] = flip(sq[column(s), :, h * DH:(h + 1) * DH])
-
-    await_others(0)
+    @pl.when(kv <= 1)
+    def _():
+        turn_queries((0, 1))
+
     pad = acc.shape[0] // n_head
     place = lax.broadcasted_iota(jnp.int32, acc.shape, 0)
+    lse = jnp.concatenate(
+        [s_max[h] * scale + jnp.log(s_sum[h]) for h in range(n_s)]
+        + [jnp.zeros((1, rows), jnp.float32)] * (pad - n_s),
+        axis=0,
+    )
+    mine = jnp.where(place // pad == hd, 2.0 * jnp.concatenate([lse] * n_head, axis=0), 0.0)
+    turn_queries((2,))
+    await_others(0, kv % 2)
     total = jnp.zeros(acc.shape, jnp.float32)
     for h in range(n_t):
         partner = inverse[h]
-        blend = mix(h)
+        blend = mix(h, kv % 2)
         own = blend[:DH] * tq_t[h].astype(jnp.float32)
         other = blend[DH:2 * DH] * sq_t[partner].astype(jnp.float32)
         mass = blend[2 * DH:2 * DH + 1]
@@ -345,12 +372,6 @@
         for s in range(1, n_head)
     ]
     start(returns)
-    lse = jnp.concatenate(
-        [s_max[h] * scale + jnp.log(s_sum[h]) for h in range(n_s)]
-        + [jnp.zeros((1, rows), jnp.float32)] * (pad - n_s),
-        axis=0,
-    )
-    mine = jnp.where(place // pad == hd, 2.0 * jnp.concatenate([lse] * n_head, axis=0), 0.0)
     side = jnp.sum(total + mine, axis=1, keepdims=True)
     across_lanes = lax.broadcasted_iota(jnp.int32, (n_head * pad, 128), 1)
     down_rows = lax.broadcasted_iota(jnp.int32, (n_head * pad, 128), 0)
@@ -404,7 +425,8 @@
         @pl.when(not_last)
         def _():
             upward(block, 0).wait_send()
-            upward(block, n_head).wait_send()
+            for piece in halves:
+                upward(block, piece).wait_send()
 
             @pl.when(block < shared)
             def _():
@@ -421,6 +443,11 @@
     ).wait()
     line = jnp.sum(sums[...], axis=0)
     loss_ref[...] = line[:, :n_s] / (n_dp * rows * n_kv)
+
+
+def finish(kl_in, loss_in, kl_ref, loss_ref):
+    kl_ref[...] = kl_in[...]
+    loss_ref[...] = loss_in[...]
 
 
 def per_device(teacher_query, teacher_key, student_query, student_key, pair_table):
@@ -454,11 +481,11 @@
             pltpu.VMEM((n_head, n_kv, rows, g_s * DH), bf16),
             pltpu.VMEM((n_t, DH, rows), bf16),
             pltpu.VMEM((HS, DH, rows), bf16),
-            pltpu.VMEM((g_t * KVS, 2 * DH + 16, rows), bf16),
-            pltpu.VMEM((n_t, rows, rows), bf16),
+            pltpu.VMEM((2, g_t * KVS, 2 * DH + 16, rows), bf16),
+            pltpu.VMEM((2, n_t, rows, rows), bf16),
             pltpu.VMEM((n_t, 2 * DH + 16, rows), f32),
             pltpu.VMEM((n_t, 1, rows), f32),
-            pltpu.VMEM((n_t, 1, rows), f32),
+            pltpu.VMEM((2, n_t, 1, rows), f32),
             pltpu.VMEM((n_s, 1, rows), f32),
             pltpu.VMEM((n_s, 1, rows), f32),
             pltpu.SMEM(pair_table.shape[::-1], jnp.int32),
@@ -476,13 +503,25 @@
             dma((3, max(n_head - 1, 1))),
             dma((max(n_head - 1, 1),)),
             dma((max(n_head - 1, 1),)),
-            dma((n_kv, n_head + 1)),
-            dma((n_kv, n_head + 1)),
+            dma((n_kv, n_head + 2)),
+            dma((n_kv, n_head + 2)),
             dma(()),
             dma(()),
         ],
         compiler_params=pltpu.CompilerParams(collective_id=0, has_side_effects=True),
     )(pair_table.T, teacher_query, teacher_key, student_query, student_key)
+    kl, loss = pl.pallas_call(
+        finish,
+        out_shape=(
+            jax.ShapeDtypeStruct((n_s, 1, rows), f32),
+            jax.ShapeDtypeStruct((1, n_s), f32),
+        ),
+        in_specs=[pl.BlockSpec(memory_space=pltpu.VMEM)] * 2,
+        out_specs=(
+            pl.BlockSpec(memory_space=pltpu.VMEM),
+            pl.BlockSpec(memory_space=pltpu.VMEM),
+        ),
+    )(pltpu.with_memory_space_constraint(kl, pltpu.VMEM), pltpu.with_memory_space_constraint(loss, pltpu.VMEM))
     return kl.reshape(1, n_s, rows), loss.reshape(n_s)
 
 

time: 30.3 us -> 29.6 us (0.977)
  local copies, waits for them, and re-layouts: 1.11 us -> 0 us
  Pallas kernels: 28.4 us -> 28.9 us
    unnamed x2 -> x0, local copies, waits for them, and re-layouts: 1.11 us -> none
    pallas_call x0 -> x1, Pallas kernels: none -> 0.6 us  [per_device(): pl.pallas_call(finish, out_shape=(jax.ShapeDtypeStruct((n_s, 1, rows), f3...]
where the time goes in v5:
time: 29.6 us; the launch traced here: 29.5 us
  Pallas kernels  28.9 us (98%)
  between operations  0.64 us (2%)
    pallas_call x1, Pallas kernels, per_device(): pl.pallas_call(functools.partial(kernel, n_dp, n_head, n_kv, rows, shared...  28.3 us
    pallas_call x1, Pallas kernels, per_device(): pl.pallas_call(finish, out_shape=(jax.ShapeDtypeStruct((n_s, 1, rows), f3...  0.6 us

profile of v5, /device:TPU:0, one launch (start us, length us, event | category | flops | bytes accessed | tf_op | source)
XLA Modules:
  0.0 29.5 jit_solution(9622090239080801429)
XLA Ops:
  0.6 28.3 %shard_map.68 = (f32[7,1,256]{2,1,0:T(1,128)S(1)}, f32[1,7]{1,0:T(1,128)S(1)}) custom-call(s32[2,14]{1,0:T(2,128)} %bitcast.3, bf16[1,256,1792]{2,1,0:T(8,128)(2,1)} %tq_hbm.1, bf16[1,256,256]{2,1,0:T(8,128)(2,1)} %tk_hbm.1, bf16[1,256,896]{2,1,0:T(8,128)(2,1)} %sq_hbm.1, bf16[1,256,128]{2,1,0:T(8,128)(2,1)} %sk_hbm.1), custom_call_target="tpu_custom_call" | custom-call | tf_op jit(solution)/shard_map/pallas_call | solution.py:466
  28.9 0.6 %shard_map.69 = (f32[7,1,256]{2,1,0:T(1,128)}, f32[1,7]{1,0:T(1,128)}) custom-call(f32[7,1,256]{2,1,0:T(1,128)S(1)} %get-tuple-element.6.kl_in, f32[1,7]{1,0:T(1,128)S(1)} %get-tuple-element.7.loss_in), custom_call_target="tpu_custom_call" | custom-call | tf_op jit(solution)/shard_map/pallas_call | solution.py:513

commit v6 on v5

--- a/solution.py
+++ b/solution.py
@@ -142,10 +142,11 @@
             land(block, 0)
             start(keys_over(block))
 
-    def receive_rest(block):
+    def receive_teacher(block):
         for piece in halves:
             land(block, piece)
 
+    def receive_student(block):
         @pl.when(block < shared)
         def _():
             land(block, 0)
@@ -174,6 +175,12 @@
 
     loads[2].wait()
     start(queries_over(0))
+
+    @pl.when(not_last)
+    def _():
+        start(queries_over(1))
+        start(queries_over(2))
+
     for s in range(1, n_head):
         greet(layer_sem, head=column(s))
 
@@ -213,7 +220,8 @@
     @pl.when(not_last & not_first)
     def _():
         receive_own(kv - 1)
-        receive_rest(kv - 1)
+        receive_teacher(kv - 1)
+        receive_student(kv - 1)
 
     visible = lax.broadcasted_iota(jnp.int32, (rows, rows), 0) <= lax.broadcasted_iota(
         jnp.int32, (rows, rows), 1
@@ -299,26 +307,45 @@
         def _():
             receive_own(kv - 1)
 
-        start(queries_over(1))
-
-        @pl.when(first)
+        @pl.when(last)
+        def _():
+            start(queries_over(1))
+
+        @pl.when(last & first)
         def _():
             start(queries_over(2))
 
     weigh_block(kv, 0, True)
     after_own()
 
+    def blend_before(s):
+        await_others(kv - s + 1, (s - 1) % 2)
+        for h in range(n_t):
+            mixed[h] = mix(h, (s - 1) % 2)
+
     def step(s, carry):
         block = kv - s
 
         @pl.when(not_last & (s < kv))
         def _():
             receive_own(block - 1)
-            receive_rest(block - 1)
+            receive_teacher(block - 1)
+
+        @pl.when(s < kv)
+        def _():
+            blend_before(s)
+
+        @pl.when(not_last & (s < kv))
+        def _():
+            receive_student(block - 1)
+
+        @pl.when(s == kv - 1)
+        def _():
+            turn_queries((0,))
 
         @pl.when((s == kv) & (s > 1))
         def _():
-            turn_queries((0, 1))
+            turn_queries((1,))
 
         weigh_block(block, s % 2, False)
 
@@ -326,13 +353,14 @@
         def _():
             receive_own(block - 1)
 
-        @pl.when(s == 1)
+        @pl.when(last & (s == 1))
         def _():
             start(queries_over(2))
 
-        await_others(block + 1, (s - 1) % 2)
-        for h in range(n_t):
-            mixed[h] = mix(h, (s - 1) % 2)
+        @pl.when(s == kv)
+        def _():
+            blend_before(s)
+
         return carry
 
     lax.fori_loop(1, kv + 1, step, 0)
@@ -442,7 +470,7 @@
         device_id={"head": column(1)}, device_id_type=MESH,
     ).wait()
     line = jnp.sum(sums[...], axis=0)
-    loss_ref[...] = line[:, :n_s] / (n_dp * rows * n_kv)
+    loss_ref[...] = line[:, :n_s] * (1.0 / (n_dp * rows * n_kv))
 
 
 def finish(kl_in, loss_in, kl_ref, loss_ref):

time: 29.6 us -> 29.3 us (0.990)
  Pallas kernels: 28.9 us -> 28.5 us
    pallas_call x1, Pallas kernels: 28.3 us -> 27.9 us  [per_device(): pl.pallas_call(functools.partial(kernel, n_dp, n_head, n_kv, rows, shared...]
where the time goes in v6:
time: 29.3 us; the launch traced here: 29.2 us
  Pallas kernels  28.5 us (97%)
  between operations  0.64 us (2%)
    pallas_call x1, Pallas kernels, per_device(): pl.pallas_call(functools.partial(kernel, n_dp, n_head, n_kv, rows, shared...  27.9 us
    pallas_call x1, Pallas kernels, per_device(): pl.pallas_call(finish, out_shape=(jax.ShapeDtypeStruct((n_s, 1, rows), f3...  0.6 us

profile of v6, /device:TPU:0, one launch (start us, length us, event | category | flops | bytes accessed | tf_op | source)
XLA Modules:
  0.0 29.2 jit_solution(8939238249556086647)
XLA Ops:
  0.6 27.9 %shard_map.68 = (f32[7,1,256]{2,1,0:T(1,128)S(1)}, f32[1,7]{1,0:T(1,128)S(1)}) custom-call(s32[2,14]{1,0:T(2,128)} %bitcast.3, bf16[1,256,1792]{2,1,0:T(8,128)(2,1)} %tq_hbm.1, bf16[1,256,256]{2,1,0:T(8,128)(2,1)} %tk_hbm.1, bf16[1,256,896]{2,1,0:T(8,128)(2,1)} %sq_hbm.1, bf16[1,256,128]{2,1,0:T(8,128)(2,1)} %sk_hbm.1), custom_call_target="tpu_custom_call" | custom-call | tf_op jit(solution)/shard_map/pallas_call | solution.py:494
  28.6 0.6 %shard_map.69 = (f32[7,1,256]{2,1,0:T(1,128)}, f32[1,7]{1,0:T(1,128)}) custom-call(f32[7,1,256]{2,1,0:T(1,128)S(1)} %get-tuple-element.6.kl_in, f32[1,7]{1,0:T(1,128)S(1)} %get-tuple-element.7.loss_in), custom_call_target="tpu_custom_call" | custom-call | tf_op jit(solution)/shard_map/pallas_call | solution.py:541

commit v7 on v6

--- a/solution.py
+++ b/solution.py
@@ -276,7 +276,7 @@
             s_sum[h] = part if diagonal else s_sum[h] * decay + part
         turn_student(hd, block, slot)
 
-    def await_others(block, slot):
+    def await_others(block):
         @pl.when((block < shared) & last & not_first & (block != kv))
         def _():
             for s in range(1, n_head):
@@ -287,12 +287,13 @@
             for copy in keys_over(block):
                 copy.wait_recv()
 
+    def turn_others(block, slot):
         for s in range(1, n_head):
             turn_student(column(s), block, slot)
 
-    def mix(h, slot):
+    def mix(h, slot, blend):
         part = nn(key_t[slot, h // per_t * KVS + inverse[h] // per_s], weights[slot, h])
-        return mixed[h] * t_decay[slot, h] + part
+        return blend * t_decay[slot, h] + part
 
     def turn_queries(groups):
         for group in groups:
@@ -319,9 +320,10 @@
     after_own()
 
     def blend_before(s):
-        await_others(kv - s + 1, (s - 1) % 2)
+        await_others(kv - s + 1)
+        turn_others(kv - s + 1, (s - 1) % 2)
         for h in range(n_t):
-            mixed[h] = mix(h, (s - 1) % 2)
+            mixed[h] = mix(h, (s - 1) % 2, mixed[h])
 
     def step(s, carry):
         block = kv - s
@@ -356,10 +358,6 @@
         @pl.when(last & (s == 1))
         def _():
             start(queries_over(2))
-
-        @pl.when(s == kv)
-        def _():
-            blend_before(s)
 
         return carry
 
@@ -377,12 +375,24 @@
         axis=0,
     )
     mine = jnp.where(place // pad == hd, 2.0 * jnp.concatenate([lse] * n_head, axis=0), 0.0)
+    @pl.when(first)
+    def _():
+        key_t[1, :, :2 * DH] = jnp.zeros((g_t * KVS, 2 * DH, rows), bf16)
+        weights[1] = jnp.zeros((n_t, rows, rows), bf16)
+        t_decay[1] = jnp.zeros((n_t, 1, rows), jnp.float32)
+
+    @pl.when(not_first)
+    def _():
+        await_others(1)
+        turn_others(1, (kv - 1) % 2)
+
+    await_others(0)
     turn_queries((2,))
-    await_others(0, kv % 2)
+    turn_others(0, kv % 2)
     total = jnp.zeros(acc.shape, jnp.float32)
     for h in range(n_t):
         partner = inverse[h]
-        blend = mix(h, kv % 2)
+        blend = mix(h, kv % 2, mix(h, (kv + 1) % 2, mixed[h]))
         own = blend[:DH] * tq_t[h].astype(jnp.float32)
         other = blend[DH:2 * DH] * sq_t[partner].astype(jnp.float32)
         mass = blend[2 * DH:2 * DH + 1]

time: 29.3 us -> 28.9 us (0.986)
  Pallas kernels: 28.5 us -> 28.1 us
    pallas_call x1, Pallas kernels: 27.9 us -> 27.5 us  [per_device(): pl.pallas_call(functools.partial(kernel, n_dp, n_head, n_kv, rows, shared...]
where the time goes in v7:
time: 28.9 us; the launch traced here: 28.7 us
  Pallas kernels  28.1 us (97%)
  between operations  0.64 us (2%)
    pallas_call x1, Pallas kernels, per_device(): pl.pallas_call(functools.partial(kernel, n_dp, n_head, n_kv, rows, shared...  27.5 us
    pallas_call x1, Pallas kernels, per_device(): pl.pallas_call(finish, out_shape=(jax.ShapeDtypeStruct((n_s, 1, rows), f3...  0.6 us

profile of v7, /device:TPU:0, one launch (start us, length us, event | category | flops | bytes accessed | tf_op | source)
XLA Modules:
  0.0 28.7 jit_solution(14242860065629764858)
XLA Ops:
  0.6 27.5 %shard_map.68 = (f32[7,1,256]{2,1,0:T(1,128)S(1)}, f32[1,7]{1,0:T(1,128)S(1)}) custom-call(s32[2,14]{1,0:T(2,128)} %bitcast.3, bf16[1,256,1792]{2,1,0:T(8,128)(2,1)} %tq_hbm.1, bf16[1,256,256]{2,1,0:T(8,128)(2,1)} %tk_hbm.1, bf16[1,256,896]{2,1,0:T(8,128)(2,1)} %sq_hbm.1, bf16[1,256,128]{2,1,0:T(8,128)(2,1)} %sk_hbm.1), custom_call_target="tpu_custom_call" | custom-call | tf_op jit(solution)/shard_map/pallas_call | solution.py:504
  28.1 0.6 %shard_map.69 = (f32[7,1,256]{2,1,0:T(1,128)}, f32[1,7]{1,0:T(1,128)}) custom-call(f32[7,1,256]{2,1,0:T(1,128)S(1)} %get-tuple-element.6.kl_in, f32[1,7]{1,0:T(1,128)S(1)} %get-tuple-element.7.loss_in), custom_call_target="tpu_custom_call" | custom-call | tf_op jit(solution)/shard_map/pallas_call | solution.py:551

commit v8 on v7

--- a/solution.py
+++ b/solution.py
@@ -386,6 +386,11 @@
         await_others(1)
         turn_others(1, (kv - 1) % 2)
 
+    for way, edge in ((0, last), (1, first)):
+        @pl.when(edge)
+        def _():
+            pl.semaphore_wait(chain_sem.at[way], 1)
+
     await_others(0)
     turn_queries((2,))
     turn_others(0, kv % 2)
@@ -409,7 +414,6 @@
         )
         for s in range(1, n_head)
     ]
-    start(returns)
     side = jnp.sum(total + mine, axis=1, keepdims=True)
     across_lanes = lax.broadcasted_iota(jnp.int32, (n_head * pad, 128), 1)
     down_rows = lax.broadcasted_iota(jnp.int32, (n_head * pad, 128), 0)
@@ -436,12 +440,8 @@
             return lax.fori_loop(0, n_dp, middle, carry)
         lax.fori_loop(0, n_kv, outer, 0)
 
-    for way, edge in ((0, last), (1, first)):
-        @pl.when(edge)
-        def _():
-            pl.semaphore_wait(chain_sem.at[way], 1)
-
     each_peer(lambda d, h, k: share(d, h, k).start())
+    start(returns)
     sums[rank] = sums_out[hd]
     kl = acc[pl.ds(hd * pad, pad)] + 2.0 * lse
     for s in range(1, n_head):

time: 28.9 us -> 28.8 us (level)
  no operation moved by 1% of the time
where the time goes in v8:
time: 28.8 us; the launch traced here: 28.7 us
  Pallas kernels  28 us (97%)
  between operations  0.64 us (2%)
    pallas_call x1, Pallas kernels, per_device(): pl.pallas_call(functools.partial(kernel, n_dp, n_head, n_kv, rows, shared...  27.4 us
    pallas_call x1, Pallas kernels, per_device(): pl.pallas_call(finish, out_shape=(jax.ShapeDtypeStruct((n_s, 1, rows), f3...  0.6 us

profile of v8, /device:TPU:0, one launch (start us, length us, event | category | flops | bytes accessed | tf_op | source)
XLA Modules:
  0.0 28.7 jit_solution(8608825174019020476)
XLA Ops:
  0.6 27.4 %shard_map.68 = (f32[7,1,256]{2,1,0:T(1,128)S(1)}, f32[1,7]{1,0:T(1,128)S(1)}) custom-call(s32[2,14]{1,0:T(2,128)} %bitcast.3, bf16[1,256,1792]{2,1,0:T(8,128)(2,1)} %tq_hbm.1, bf16[1,256,256]{2,1,0:T(8,128)(2,1)} %tk_hbm.1, bf16[1,256,896]{2,1,0:T(8,128)(2,1)} %sq_hbm.1, bf16[1,256,128]{2,1,0:T(8,128)(2,1)} %sk_hbm.1), custom_call_target="tpu_custom_call" | custom-call | tf_op jit(solution)/shard_map/pallas_call | solution.py:504
  28.1 0.6 %shard_map.69 = (f32[7,1,256]{2,1,0:T(1,128)}, f32[1,7]{1,0:T(1,128)}) custom-call(f32[7,1,256]{2,1,0:T(1,128)S(1)} %get-tuple-element.6.kl_in, f32[1,7]{1,0:T(1,128)S(1)} %get-tuple-element.7.loss_in), custom_call_target="tpu_custom_call" | custom-call | tf_op jit(solution)/shard_map/pallas_call | solution.py:551
